TPU v7x, 256 devices: a whole 4x4x8 slice. The times are simulated.
256 devices in a mesh: fsdp: 32 (over y, x, z_lo), rep: 8 (over z_hi, core).
Axes of the slice: x: 4, y: 4, z: 8 (z_hi: 4, z_lo: 2; z = z_hi * 2 + z_lo), core: 2. Of those that a mesh axis runs over, the one named last changes fastest.
Arguments:
- tokens: bfloat16 [122880, 3584], P(('fsdp', 'rep')), may hold values from -6 to 6
- positions: int32 [122880], P(('fsdp', 'rep')), may hold values from 0 to 4095
- slow_weight: float32 [3584, 4096], P('fsdp', 'rep'), may hold values from -0.09375 to 0.09375
- fast_weight: bfloat16 [8, 3584, 4096], P('rep', 'fsdp'), may hold values from -0.125 to 0.125
- slow_gain: float32 [3584], P(('fsdp', 'rep')), may hold values from -3 to 3
- fast_gain: bfloat16 [8, 3584], P('rep', 'fsdp'), may hold values from -3 to 3
Outputs:
- query_states: bfloat16 [122880, 2048], P(('fsdp', 'rep'))
- key_states: bfloat16 [122880, 1024], P(('fsdp', 'rep'))
- value_states: bfloat16 [122880, 1024], P(('fsdp', 'rep'))
- new_weight: float32 [3584, 4096], P('fsdp', 'rep')
- new_gain: float32 [3584], P(('fsdp', 'rep'))
All inputs are finite; a program needn't handle non-finite values.
Results may differ from a plain program's by a relative error of at most 0.012.
Values may be sent and summed in bfloat16 or wider, within the bound.
A program may use at most 128 MiB of HBM per device.

v0:
```python
import jax
import jax.numpy as jnp
from jax import lax
from jax.sharding import PartitionSpec as P

QHEADS = 8
KVHEADS = 4
HEAD = 256
EPSILON = 1e-06
ADVANCE_RATE = 0.5
ROPE_BASE = 10000.0


def cut_along(x, dim, devices):
    lengths = x.shape
    tiles = x.reshape(*lengths[:dim], devices, lengths[dim] // devices, *lengths[dim + 1 :])
    return jnp.moveaxis(tiles, dim, 0)


def one_scatter(arrays, axis, dims):
    devices = lax.axis_size(axis)
    tiles = [cut_along(a, dim, devices) for a, dim in zip(arrays, dims)]
    lines = jnp.concatenate([b.reshape(devices, -1) for b in tiles], axis=1)
    width = max(16, -(-lines.shape[1] // 1024) * 8)
    lines = jnp.pad(lines, ((0, 0), (0, width * 128 - lines.shape[1]))).reshape(-1, 128)
    line, at, done = (lax.psum_scatter(lines, axis, tiled=True).reshape(-1), 0, [])
    for b in tiles:
        part = b[0]
        done.append(line[at : at + part.size].reshape(part.shape))
        at += part.size
    return tuple(done)


def rotate(values, positions, head_count):
    row_count = values.shape[0]
    head_width = values.shape[1] // head_count
    half_width = head_width // 2
    by_head = values.reshape(row_count, head_count, head_width)
    inverse_rates = ROPE_BASE ** (-(jnp.arange(half_width, dtype=jnp.float32) * 2.0 / head_width))
    angles = positions.astype(jnp.float32)[:, None] * inverse_rates[None, :]
    cosine_table = jnp.cos(angles)[:, None, :]
    sine_table = jnp.sin(angles)[:, None, :]
    front_half = by_head[:, :, :half_width]
    back_half = by_head[:, :, half_width:]
    turned = jnp.concatenate(
        [
            front_half * cosine_table - back_half * sine_table,
            back_half * cosine_table + front_half * sine_table,
        ],
        axis=2,
    )
    return turned.reshape(row_count, head_count * head_width)


def on_device(tokens, positions, slow_weight, fast_weight, slow_gain, fast_gain):
    replicas = lax.axis_size("rep")
    totals = tuple(
        (
            part.astype(jnp.float32)
            for part in one_scatter(
                (
                    fast_weight.astype(jnp.float32).astype(jnp.bfloat16),
                    fast_gain.astype(jnp.float32).astype(jnp.bfloat16),
                ),
                "rep",
                (2, 1),
            )
        )
    )
    new_weight = slow_weight + ADVANCE_RATE * (totals[0][0] / replicas - slow_weight)
    new_gain = slow_gain + ADVANCE_RATE * (totals[1][0] / replicas - slow_gain)
    own_weight = new_weight.astype(jnp.bfloat16)
    own_gain = new_gain.astype(jnp.bfloat16)
    floats = tokens.astype(jnp.float32)
    inv_rms = lax.rsqrt(jnp.mean(floats * floats, axis=1, keepdims=True) + EPSILON)
    column_weight = lax.all_gather(own_weight, "fsdp", axis=0, tiled=True)
    whole_gain = lax.all_gather(own_gain, ("fsdp", "rep"), axis=0, tiled=True)
    normed = (floats * inv_rms * (1.0 + whole_gain.astype(jnp.float32))[None, :]).astype(
        jnp.bfloat16
    )
    projected = jnp.dot(
        normed,
        lax.all_gather(column_weight, "rep", axis=1, tiled=True),
        preferred_element_type=jnp.float32,
    )
    query_cols = QHEADS * HEAD
    key_cols = KVHEADS * HEAD
    query_states = rotate(projected[:, :query_cols], positions, QHEADS).astype(jnp.bfloat16)
    key_states = rotate(
        projected[:, query_cols : query_cols + key_cols], positions, KVHEADS
    ).astype(jnp.bfloat16)
    value_states = projected[:, query_cols + key_cols :].astype(jnp.bfloat16)
    return (query_states, key_states, value_states, new_weight, new_gain)


def solution(mesh):
    return jax.shard_map(
        on_device,
        mesh=mesh,
        in_specs=(
            P(("fsdp", "rep"), None),
            P(("fsdp", "rep")),
            P("fsdp", "rep"),
            P("rep", "fsdp", None),
            P(("fsdp", "rep")),
            P("rep", "fsdp"),
        ),
        out_specs=(
            P(("fsdp", "rep"), None),
            P(("fsdp", "rep"), None),
            P(("fsdp", "rep"), None),
            P("fsdp", "rep"),
            P(("fsdp", "rep")),
        ),
        check_vma=False,
    )
```

profile of v0, /device:TPU:35, one launch (start us, length us, event | category | flops | bytes accessed | tf_op | source)
XLA Modules:
  0.0 565.5 jit_solution(11715870747473245055)
XLA Ops:
  7.2 1.5 copy.11
  9.2 1.3 reduce.3
  10.7 1.4 reshape.107
  12.2 0.6 dynamic-slice
  13.8 75.9 %all-reduce.5.cloned.1.call-done = bf16[3648,128]{1,0:T(8,128)(2,1)} async-done(((bf16[3648,128]{1,0:T(8,128)(2,1)}), bf16[3648,128]{1,0:T(8,128)(2,1)}) %all-reduce.5.cloned.1.call-update) | async-done | bytes 933904
  89.7 1.6 convert_multiply_fusion.2
  91.3 1.7 div.28
  92.9 1.8 fusion.13
  94.8 141.0 %all-gather.3.cloned.1.call-done = bf16[3584,512]{1,0:T(8,128)(2,1)} async-done(((bf16[112,512]{1,0:T(8,128)(2,1)}), bf16[3584,512]{1,0:T(8,128)(2,1)}) %all-gather.3.cloned.1.call-update) | async-done | bytes 3670032 | tf_op jit(solution)/shard_map/all_gather | solution.py:76
  235.9 0.7 fusion
  236.6 1.7 multiply_cosine_fusion
  238.3 0.9 dynamic-slice_bitcast_fusion
  239.9 109.2 %all-reduce.1 = bf16[3584]{0:T(1024)(128)(2,1)S(1)} all-reduce(bf16[3584]{0:T(1024)(128)(2,1)S(1)} %dynamic-update-slice), channel_id=1, replica_groups=mesh['fsdp'=32,'rep'=8] {'fsdp','rep'}, use_global_device_ids=true, to_apply=%add.1 | all-reduce | flops 3584 | bytes 14336
  349.2 176.8 %all-gather.5.cloned.1.call-done = bf16[3584,4096]{1,0:T(8,128)(2,1)} async-done(((bf16[3584,512]{1,0:T(8,128)(2,1)}), bf16[3584,4096]{1,0:T(8,128)(2,1)}) %all-gather.5.cloned.1.call-update) | async-done | bytes 29360144 | tf_op jit(solution)/shard_map/all_gather | solution.py:83
  526.0 19.2 %fusion.3 = f32[480,4096]{1,0:T(8,128)S(1)} fusion(bf16[3584,4096]{1,0:T(8,128)(2,1)} %all-gather.5.cloned.1.call-done, bf16[480,3584]{1,0:T(8,128)(2,1)} %param.6, f32[3584]{0:T(1024)S(1)} %convert_add_fusion, f32[480]{0:T(512)S(1)} %add_rsqrt_fusion), kind=kOutput, calls=%fused_computation.5 | convolution fusion | flops 14099742720 | bytes 40681344 | tf_op jit(solution)/shard_map/dot_general | solution.py:81
  545.2 1.5 slice.42
  546.7 2.1 copy-done
  548.9 1.1 slice.62
  550.0 2.2 reshape.110
  552.2 0.5 subtract_convert_fusion.1
  553.3 1.1 copy.14
  554.4 1.8 copy.12
  556.2 0.6 subtract_convert_fusion
  557.1 1.9 copy.13
  (31 shorter events, 2.3 us)
Async XLA Ops:
  7.2 5.0 copy-start.5
  7.2 82.5 %all-reduce.5.cloned.1.call-start = ((), (), s32[]{:S(2)}) async-start(), calls=%async_computation.2 | async-start | bytes 1867776
  12.1 223.7 %copy-start.3 = (s32[480]{0:T(512)S(1)}, s32[480]{0:T(512)}, u32[]{:S(2)}) copy-start(s32[480]{0:T(512)} %param.7) | copy-start | bytes 5764
  12.1 223.8 %copy-start.1 = (bf16[480,3584]{1,0:T(8,128)(2,1)S(1)}, bf16[480,3584]{1,0:T(8,128)(2,1)}, u32[]{:S(2)}) copy-start(bf16[480,3584]{1,0:T(8,128)(2,1)} %param.6) | copy-start | bytes 10321924
  12.1 223.7 %all-gather.3.cloned.1.call-start = ((), (), s32[]{:S(2)}) async-start(), calls=%async_computation | async-start | bytes 3784704 | tf_op jit(solution)/shard_map/all_gather | solution.py:76
  94.8 431.2 %all-gather.5.cloned.1.call-start = ((), (), s32[]{:S(2)}) async-start(), calls=%async_computation.1 | async-start | bytes 33030144 | tf_op jit(solution)/shard_map/all_gather | solution.py:83
  235.8 3.5 copy-start.4
  545.2 3.7 copy-start
  550.0 2.2 copy-start.2
  552.2 2.2 slice-start
Sparse Core Ops, SparseCore 0:
  12.2 77.4 all-reduce.4
  94.9 140.8 all-gather.2
  237.6 288.3 all-gather.4
where the time goes:
time: 566 us
  waiting for transfers between devices  394 us (70%)
  blocking collectives  109 us (19%)
  matrix products  19.2 us (3%)
  local copies, waits for them, and re-layouts  18.6 us (3%)
  between operations  14.9 us (3%)
  other arithmetic  9.67 us (2%)
    all_gather x1, waiting for transfers between devices, on_device(): lax.all_gather(column_weight, 'rep', axis=1, tiled=True)  177 us
    all_gather x1, waiting for transfers between devices, on_device(): column_weight = lax.all_gather(own_weight, 'fsdp', axis=0, tiled=True)  141 us
    unnamed x1, blocking collectives  109 us
    unnamed x4, waiting for transfers between devices  76 us
    dot_general x1, matrix products, on_device(): jnp.dot(normed, lax.all_gather(column_weight, 'rep', axis=1, tiled=True),...  19.2 us
  transfers between devices with their start and end apart: 3, of which 3 were waited for; matrix products, arithmetic and copies ran while one was open for 1% of the time, Pallas kernels for 0%

commit v1 on v0

--- a/solution.py
+++ b/solution.py
@@ -9,6 +9,12 @@
 EPSILON = 1e-06
 ADVANCE_RATE = 0.5
 ROPE_BASE = 10000.0
+
+
+def gathered_along(x, mesh_axis, dim):
+    parts = lax.all_gather(x, mesh_axis, axis=0, tiled=False)
+    whole = jnp.concatenate(parts, axis=dim)
+    return whole
 
 
 def cut_along(x, dim, devices):
@@ -79,9 +85,7 @@
         jnp.bfloat16
     )
     projected = jnp.dot(
-        normed,
-        lax.all_gather(column_weight, "rep", axis=1, tiled=True),
-        preferred_element_type=jnp.float32,
+        normed, gathered_along(column_weight, "rep", 1), preferred_element_type=jnp.float32
     )
     query_cols = QHEADS * HEAD
     key_cols = KVHEADS * HEAD

time: 566 us -> 607 us (1.072)
  local copies, waits for them, and re-layouts: 18.6 us -> 54.6 us
    reshape x0 -> x1, local copies, waits for them, and re-layouts: none -> 36 us  [gathered_along(): whole = jnp.concatenate(parts, axis=dim)]
where the time goes in v1:
time: 607 us; the launch traced here: 606 us
  waiting for transfers between devices  392 us (65%)
  blocking collectives  111 us (18%)
  local copies, waits for them, and re-layouts  54.6 us (9%)
  matrix products  21.9 us (4%)
  between operations  14.9 us (2%)
  other arithmetic  11.1 us (2%)
    all_gather x1, waiting for transfers between devices, gathered_along(): parts = lax.all_gather(x, mesh_axis, axis=0, tiled=False)  175 us
    all_gather x1, waiting for transfers between devices, on_device(): column_weight = lax.all_gather(own_weight, 'fsdp', axis=0, tiled=True)  141 us
    unnamed x1, blocking collectives  111 us
    unnamed x4, waiting for transfers between devices  76 us
    reshape x1, local copies, waits for them, and re-layouts, gathered_along(): whole = jnp.concatenate(parts, axis=dim)  36 us
    dot_general x1, matrix products, on_device(): jnp.dot(normed, gathered_along(column_weight, 'rep', 1), preferred_elemen...  21.9 us
  transfers between devices with their start and end apart: 3, of which 3 were waited for; matrix products, arithmetic and copies ran while one was open for 1% of the time, Pallas kernels for 0%

profile of v1, /device:TPU:35, one launch (start us, length us, event | category | flops | bytes accessed | tf_op | source)
XLA Modules:
  0.0 605.6 jit_solution(3037273100259408362)
XLA Ops:
  7.7 1.3 reduce.3
  9.1 1.5 copy.13
  10.7 1.4 reshape.113
  12.2 0.6 dynamic-slice
  13.8 75.9 %all-reduce.5.cloned.1.call-done = bf16[3648,128]{1,0:T(8,128)(2,1)} async-done(((bf16[3648,128]{1,0:T(8,128)(2,1)}), bf16[3648,128]{1,0:T(8,128)(2,1)}) %all-reduce.5.cloned.1.call-update) | async-done | bytes 933904
  89.7 1.6 convert_multiply_fusion.2
  91.3 1.7 div.28
  92.9 1.8 fusion.13
  94.8 141.0 %all-gather.4.cloned.1.call-done = bf16[3584,512]{1,0:T(8,128)(2,1)} async-done(((bf16[112,512]{1,0:T(8,128)(2,1)}), bf16[3584,512]{1,0:T(8,128)(2,1)}) %all-gather.4.cloned.1.call-update) | async-done | bytes 3670032 | tf_op jit(solution)/shard_map/all_gather | solution.py:82
  235.9 0.7 fusion
  236.6 1.7 multiply_cosine_fusion
  238.4 0.9 dynamic-slice_bitcast_fusion
  240.0 110.7 %all-reduce.1 = bf16[3584]{0:T(1024)(128)(2,1)S(1)} all-reduce(bf16[3584]{0:T(1024)(128)(2,1)S(1)} %dynamic-update-slice), channel_id=1, replica_groups=mesh['fsdp'=32,'rep'=8] {'fsdp','rep'}, use_global_device_ids=true, to_apply=%add.1 | all-reduce | flops 3584 | bytes 14336
  350.7 175.3 %all-gather.6.cloned.1.call-done = bf16[28672,512]{1,0:T(8,128)(2,1)} async-done(((bf16[3584,512]{1,0:T(8,128)(2,1)}), bf16[28672,512]{1,0:T(8,128)(2,1)}) %all-gather.6.cloned.1.call-update) | async-done | bytes 29360144 | tf_op jit(solution)/shard_map/all_gather | solution.py:15
  526.0 36.0 %copy.12 = bf16[3584,8,512]{0,2,1:T(8,128)(2,1)} copy(bf16[3584,8,512]{2,0,1:T(8,128)(2,1)} %bitcast.22) | data formatting | bytes 58720256 | tf_op jit(solution)/shard_map/reshape | solution.py:16
  562.0 21.9 %fusion.3 = f32[480,4096]{1,0:T(8,128)} fusion(bf16[3584,4096]{0,1:T(8,128)(2,1)} %bitcast.23, bf16[480,3584]{1,0:T(8,128)(2,1)S(1)} %copy-done, f32[3584]{0:T(1024)S(1)} %convert_add_fusion, f32[480]{0:T(512)S(1)} %add_rsqrt_fusion), kind=kOutput, calls=%fused_computation.5 | convolution fusion | flops 14099742720 | bytes 40681344 | tf_op jit(solution)/shard_map/dot_general | solution.py:87
  584.0 2.6 slice.62
  586.6 2.1 slice-done.1
  588.7 1.8 copy.14
  591.3 1.9 copy.15
  593.2 2.2 reshape.118
  595.4 2.0 subtract_convert_fusion.1
  597.4 0.5 pad_maximum_fusion.1
  597.9 1.1 copy.16
  (33 shorter events, 2.3 us)
Async XLA Ops:
  7.2 5.0 copy-start.5
  7.2 82.5 %all-reduce.5.cloned.1.call-start = ((), (), s32[]{:S(2)}) async-start(), calls=%async_computation.2 | async-start | bytes 1867776
  12.1 223.7 %copy-start.3 = (s32[480]{0:T(512)S(1)}, s32[480]{0:T(512)}, u32[]{:S(2)}) copy-start(s32[480]{0:T(512)} %param.7) | copy-start | bytes 5764
  12.1 223.8 %copy-start = (bf16[480,3584]{1,0:T(8,128)(2,1)S(1)}, bf16[480,3584]{1,0:T(8,128)(2,1)}, u32[]{:S(2)}) copy-start(bf16[480,3584]{1,0:T(8,128)(2,1)} %param.6) | copy-start | bytes 10321924
  12.1 223.7 %all-gather.4.cloned.1.call-start = ((), (), s32[]{:S(2)}) async-start(), calls=%async_computation | async-start | bytes 3784704 | tf_op jit(solution)/shard_map/all_gather | solution.py:82
  94.8 431.2 %all-gather.6.cloned.1.call-start = ((), (), s32[]{:S(2)}) async-start(), calls=%async_computation.1 | async-start | bytes 33030144 | tf_op jit(solution)/shard_map/all_gather | solution.py:15
  235.8 3.5 copy-start.4
  586.6 2.1 slice-start.1
  588.7 1.8 copy-start.1
  588.7 1.8 copy-start.2
  591.1 2.1 slice-start
Sparse Core Ops, SparseCore 0:
  12.2 77.4 all-reduce.4
  94.9 140.8 all-gather.3
  237.6 288.3 all-gather.5

commit v2 on v0

--- a/solution.py
+++ b/solution.py
@@ -73,7 +73,10 @@
     own_gain = new_gain.astype(jnp.bfloat16)
     floats = tokens.astype(jnp.float32)
     inv_rms = lax.rsqrt(jnp.mean(floats * floats, axis=1, keepdims=True) + EPSILON)
-    column_weight = lax.all_gather(own_weight, "fsdp", axis=0, tiled=True)
+    n_dev = lax.axis_size("fsdp")
+    blocks = jnp.stack([own_weight for _ in range(n_dev)])
+    blocks = lax.all_to_all(blocks, "fsdp", split_axis=0, concat_axis=0)
+    column_weight = jnp.concatenate(blocks, axis=0)
     whole_gain = lax.all_gather(own_gain, ("fsdp", "rep"), axis=0, tiled=True)
     normed = (floats * inv_rms * (1.0 + whole_gain.astype(jnp.float32))[None, :]).astype(
         jnp.bfloat16

time: 566 us -> 447 us (0.79)
  waiting for transfers between devices: 394 us -> 246 us
  blocking collectives: 109 us -> 139 us
    all_gather x1 -> x0, waiting for transfers between devices: 141 us -> none  [on_device(): column_weight = lax.all_gather(own_weight, 'fsdp', axis=0, tiled=True)]
    all_to_all x0 -> x1, blocking collectives: none -> 49.9 us  [on_device(): blocks = lax.all_to_all(blocks, 'fsdp', split_axis=0, concat_axis=0)]
    unnamed x1, blocking collectives: 109 us -> 89.3 us
    all_gather x1, waiting for transfers between devices: 177 us -> 170 us  [on_device(): lax.all_gather(column_weight, 'rep', axis=1, tiled=True)]
    unnamed x20 -> x22, local copies, waits for them, and re-layouts: 9.83 us -> 11.8 us
    unnamed x4 -> x3, waiting for transfers between devices: 76 us -> 76.3 us
  transfers between devices with their start and end apart: 3 -> 2, of which waited for: 3 -> 2; matrix products, arithmetic and copies ran while one was open for 1% -> 1% of each run, Pallas kernels for 0% -> 0%
where the time goes in v2:
time: 447 us
  waiting for transfers between devices  246 us (55%)
  blocking collectives  139 us (31%)
  local copies, waits for them, and re-layouts  19.4 us (4%)
  matrix products  19.2 us (4%)
  between operations  14.8 us (3%)
  other arithmetic  7.9 us (2%)
    all_gather x1, waiting for transfers between devices, on_device(): lax.all_gather(column_weight, 'rep', axis=1, tiled=True)  170 us
    unnamed x1, blocking collectives  89.3 us
    unnamed x3, waiting for transfers between devices  76.3 us
    all_to_all x1, blocking collectives, on_device(): blocks = lax.all_to_all(blocks, 'fsdp', split_axis=0, concat_axis=0)  49.9 us
    dot_general x1, matrix products, on_device(): jnp.dot(normed, lax.all_gather(column_weight, 'rep', axis=1, tiled=True),...  19.2 us
    unnamed x22, local copies, waits for them, and re-layouts  11.8 us
  transfers between devices with their start and end apart: 2, of which 2 were waited for; matrix products, arithmetic and copies ran while one was open for 1% of the time, Pallas kernels for 0%

profile of v2, /device:TPU:35, one launch (start us, length us, event | category | flops | bytes accessed | tf_op | source)
XLA Modules:
  0.0 446.7 jit_solution(7679281555094527782)
XLA Ops:
  7.2 1.5 copy.11
  9.3 1.3 reduce.3
  10.8 1.4 reshape.112
  12.2 0.6 dynamic-slice
  13.5 76.3 %all-reduce.5.cloned.1.call-done = bf16[3648,128]{1,0:T(8,128)(2,1)} async-done(((bf16[3648,128]{1,0:T(8,128)(2,1)}), bf16[3648,128]{1,0:T(8,128)(2,1)}) %all-reduce.5.cloned.1.call-update) | async-done | bytes 933904
  89.7 0.9 convert_multiply_fusion.2
  90.7 0.7 fusion.13
  91.8 49.9 %all_to_all.5 = bf16[32,112,512]{2,1,0:T(8,128)(2,1)} all-to-all(bf16[32,112,512]{2,1,0:T(8,128)(2,1)S(1)} %stack.2), channel_id=1, replica_groups=mesh['fsdp'=32,'rep'=8] {'fsdp'}, dimensions={0} | all-to-all | bytes 7340032 | tf_op jit(solution)/shard_map/all_to_all | solution.py:78
  141.8 0.6 copy-done.4
  142.4 1.3 copy-done.1
  143.7 0.7 fusion
  144.5 1.7 multiply_cosine_fusion
  146.2 0.9 dynamic-slice_bitcast_fusion
  147.8 89.3 %all-reduce.1 = bf16[3584]{0:T(1024)(128)(2,1)S(1)} all-reduce(bf16[3584]{0:T(1024)(128)(2,1)S(1)} %dynamic-update-slice), channel_id=1, replica_groups=mesh['fsdp'=32,'rep'=8] {'fsdp','rep'}, use_global_device_ids=true, to_apply=%add.1 | all-reduce | flops 3584 | bytes 14336
  237.1 169.8 %all-gather.2.cloned.1.call-done = bf16[3584,4096]{1,0:T(8,128)(2,1)} async-done(((bf16[3584,512]{1,0:T(8,128)(2,1)}), bf16[3584,4096]{1,0:T(8,128)(2,1)}) %all-gather.2.cloned.1.call-update) | async-done | bytes 29360144 | tf_op jit(solution)/shard_map/all_gather | solution.py:86
  406.9 19.2 %fusion.3 = f32[480,4096]{1,0:T(8,128)S(1)} fusion(bf16[3584,4096]{1,0:T(8,128)(2,1)} %all-gather.2.cloned.1.call-done, bf16[480,3584]{1,0:T(8,128)(2,1)} %param.6, f32[3584]{0:T(1024)S(1)} %convert_add_fusion, f32[480]{0:T(512)S(1)} %add_rsqrt_fusion), kind=kOutput, calls=%fused_computation.5 | convolution fusion | flops 14099742720 | bytes 40681344 | tf_op jit(solution)/shard_map/dot_general | solution.py:84
  426.1 1.5 slice.42
  427.6 2.1 copy-done
  429.7 1.1 slice.62
  430.8 2.2 reshape.116
  434.1 1.1 copy.14
  435.3 1.8 copy.12
  437.1 0.6 subtract_convert_fusion
  437.9 1.9 copy.13
  (32 shorter events, 3.3 us)
Async XLA Ops:
  7.2 5.0 %copy-start.6 = (u32[256]{0:T(256)S(1)}, u32[256]{0:T(256)}, u32[]{:S(2)}) copy-start(u32[256]{0:T(256)} %constant.41) | copy-start | bytes 3076
  7.2 82.5 %all-reduce.5.cloned.1.call-start = ((), (), s32[]{:S(2)}) async-start(), calls=%async_computation.2 | async-start | bytes 1867776
  7.2 83.5 %copy-start.3 = (f32[112,512]{1,0:T(8,128)S(1)}, f32[112,512]{1,0:T(8,128)}, u32[]{:S(2)}) copy-start(f32[112,512]{1,0:T(8,128)} %param.8) | copy-start | bytes 688132
  12.2 394.7 %all-gather.2.cloned.1.call-start = ((), (), s32[]{:S(2)}) async-start(), calls=%async_computation.1 | async-start | bytes 33030144 | tf_op jit(solution)/shard_map/all_gather | solution.py:86
  141.7 0.7 copy-start.4
  141.7 2.0 copy-start.1
  141.7 5.4 %copy-start.5 = (f32[14]{0:T(128)S(1)}, f32[14]{0:T(128)}, u32[]{:S(2)}) copy-start(f32[14]{0:T(128)} %param.10) | copy-start | bytes 172
  426.1 3.6 copy-start
  430.8 2.2 copy-start.2
  433.0 2.2 slice-start
Sparse Core Ops, SparseCore 0:
  12.3 77.4 all-reduce.4
  141.9 264.9 all-gather.1
